TPU v7x, 8 devices: a whole 2x2x1 slice. The times are simulated.
8 devices in a mesh: data: 8 (over z, y, x, core).
Axes of the slice: x: 2, y: 2, z: 1, core: 2. Of those that a mesh axis runs over, the one named last changes fastest.
Arguments:
- tokens: bfloat16 [32768, 192], P('data')
- w_in: bfloat16 [192, 768], replicated
- w_out: bfloat16 [768, 192], replicated
- task_heads: bfloat16 [2, 192, 10], replicated
- labels: int32 [2, 32768], P(None, 'data')
- label_mask: int32 [2, 32768], P(None, 'data')
Outputs:
- output 1: float32 [2], replicated
- output 2: float32 [147456], P('data')
- output 3: float32 [147456], P('data')
All inputs are finite; a program needn't handle non-finite values.
Results may differ from a plain program's by a relative error of at most 0.00622191.
Values are sent between devices in bfloat16 or wider.
A program may use at most 1 GiB of HBM per device.

v0:
```python
import jax
import jax.numpy as jnp
from jax import lax
from jax.sharding import PartitionSpec as P

SOLVER_STEPS = 20


def device_grads(x_loc, w_in, w_out, task_heads, lab_loc, mask_loc):
    pre_act = jnp.dot(x_loc, w_in, preferred_element_type=jnp.float32)
    act_out, gelu_slope = jax.jvp(jax.nn.gelu, (pre_act,), (jnp.ones_like(pre_act),))
    act_bf = act_out.astype(jnp.bfloat16)
    residual = x_loc.astype(jnp.float32) + jnp.dot(act_bf, w_out, preferred_element_type=jnp.float32)
    z_bf = residual.astype(jnp.bfloat16)
    logits = jnp.einsum("bd,tdc->tbc", z_bf, task_heads, preferred_element_type=jnp.float32)
    soft_prob = jax.nn.softmax(logits, axis=-1)
    class_ids = jnp.arange(logits.shape[-1])
    onehot = (lab_loc[:, :, None] == class_ids).astype(jnp.float32)
    d_logit = (mask_loc[:, :, None].astype(jnp.float32) * (soft_prob - onehot)).astype(jnp.bfloat16)
    d_resid = jnp.einsum("tbc,tdc->tbd", d_logit, task_heads, preferred_element_type=jnp.float32).astype(jnp.bfloat16)
    grad_w_out = jnp.einsum("bf,tbd->tfd", act_bf, d_resid, preferred_element_type=jnp.float32)
    d_act = jnp.einsum("tbd,fd->tbf", d_resid, w_out, preferred_element_type=jnp.float32)
    d_pre = (d_act * gelu_slope[None]).astype(jnp.bfloat16)
    grad_w_in = jnp.einsum("bd,tbf->tdf", x_loc, d_pre, preferred_element_type=jnp.float32)
    return grad_w_in, grad_w_out


def gram_of(grad_rows):
    return jnp.einsum("tk,sk->ts", grad_rows, grad_rows, precision=lax.Precision.HIGHEST, preferred_element_type=jnp.float32)


def solve_weights(gram_mat):
    num_tasks = gram_mat.shape[0]
    step_scale = jnp.trace(gram_mat) / num_tasks

    def solver_step(step_idx, weights):
        pull_vec = (gram_mat * weights[None, :]).sum(axis=1)
        raised = weights * jnp.exp(-pull_vec / step_scale)
        return raised / raised.sum()

    init_weights = jnp.full((num_tasks,), 1.0 / num_tasks, jnp.float32)
    return lax.fori_loop(0, SOLVER_STEPS, solver_step, init_weights)


def solution(mesh):
    group_size = mesh.shape["data"]

    def local_step(x_loc, w_in, w_out, task_heads, lab_loc, mask_loc):
        num_tasks = task_heads.shape[0]
        label_count = lax.psum(mask_loc.sum(axis=1), "data")
        inv_count = 1.0 / jnp.maximum(label_count, 1).astype(jnp.float32)
        grad_w_in, grad_w_out = device_grads(x_loc, w_in, w_out, task_heads, lab_loc, mask_loc)
        shards = []
        for grad_full in (grad_w_in, grad_w_out):
            scaled = (grad_full.reshape(num_tasks, group_size, -1) * inv_count[:, None, None]).astype(jnp.bfloat16)
            arrived = lax.all_to_all(scaled, "data", 1, 1, tiled=True)
            shards.append(arrived.sum(axis=1, dtype=jnp.float32))
        gram_mat = lax.psum(gram_of(shards[0]) + gram_of(shards[1]), "data")
        weights = solve_weights(gram_mat)
        grad_in = (weights[:, None] * shards[0]).sum(axis=0)
        grad_out = (weights[:, None] * shards[1]).sum(axis=0)
        return weights, grad_in, grad_out

    return jax.shard_map(local_step, mesh=mesh, in_specs=(P("data", None), P(), P(), P(), P(None, "data"), P(None, "data")), out_specs=(P(), P("data"), P("data")), check_vma=False)
```

profile of v0, /device:TPU:0, one launch (start us, length us, event | category | flops | bytes accessed | tf_op | source)
XLA Modules:
  0.0 154.7 jit_solution(15153356031562767885)
XLA Ops:
  0.6 1.0 fusion.43
  1.7 13.2 %multiply_convert_fusion.2 = (bf16[4096,768]{1,0:T(8,128)(2,1)}, f32[4096,768]{1,0:T(8,128)}) fusion(bf16[4096,192]{0,1:T(8,128)(2,1)} %param.8, bf16[192,768]{1,0:T(8,128)(2,1)S(1)} %copy-done), kind=kOutput, calls=%fused_computation.21 | convolution fusion | flops 1264582656 | bytes 20742144 | tf_op jit(solution)/shard_map/dot_general | solution.py:10
  14.8 6.0 %convolution_bitcast_fusion = f32[2,4096,10]{1,2,0:T(8,128)} fusion(bf16[4096,768]{1,0:T(8,128)(2,1)} %get-tuple-element.53, bf16[768,192]{0,1:T(8,128)(2,1)S(1)} %copy-done.4, bf16[4096,192]{0,1:T(8,128)(2,1)S(1)} %copy-done.2, bf16[2,192,10]{1,0,2:T(2,128)(2,1)S(1)} %copy-done.7), kind=kOutput, calls=%fused_computation.34 | convolution fusion | flops 1241776128 | bytes 8494592 | tf_op jit(solution)/shard_map/bd,tdc->tbc/dot_general | solution.py:15
  20.8 2.2 %convolution_convert_fusion = bf16[2,4096,192]{1,2,0:T(8,128)(2,1)S(1)} fusion(s32[2,4096]{1,0:T(2,128)S(1)} %copy-done.6, f32[2,4096]{1,0:T(2,128)S(1)} %get-tuple-element.56, bf16[2,192,10]{1,0,2:T(2,128)(2,1)S(1)} %copy-done.7, f32[2,4096,10]{1,2,0:T(8,128)} %convolution_bitcast_fusion), kind=kOutput, calls=%fused_computation.25 | convolution fusion | flops 33619984 | bytes 3546624 | tf_op jit(solution)/shard_map/tbc,tdc->tbd/dot_general | solution.py:20
  23.1 1.7 %copy-done.1 = bf16[2,4096,192]{1,2,0:T(8,128)(2,1)} copy-done((bf16[2,4096,192]{1,2,0:T(8,128)(2,1)}, bf16[2,4096,192]{1,2,0:T(8,128)(2,1)S(1)}, u32[]{:S(2)}) %copy-start.1) | copy-done | bytes 3145752
  24.8 6.4 %fusion.30 = f32[2,768,192]{1,2,0:T(8,128)} fusion(bf16[2,4096,192]{1,2,0:T(8,128)(2,1)S(1)} %convolution_convert_fusion, bf16[4096,768]{1,0:T(8,128)(2,1)} %get-tuple-element.53), kind=kOutput, calls=%fused_computation.38 | convolution fusion | flops 2415919104 | bytes 10616832 | tf_op jit(solution)/shard_map/bf,tbd->tfd/dot_general | solution.py:21
  31.2 1.9 %copy.22 = f32[2,768,192]{2,1,0:T(8,128)S(1)} copy(f32[2,768,192]{1,2,0:T(8,128)} %fusion.30) | data formatting | bytes 2359296 | tf_op jit(solution)/shard_map/bf,tbd->tfd/transpose | solution.py:21
  33.0 1.7 %reshape.22 = f32[2,8,18432]{2,1,0:T(8,128)} reshape(f32[2,768,192]{2,1,0:T(8,128)S(1)} %copy.22) | data formatting | bytes 2359296 | tf_op jit(solution)/shard_map/reshape | solution.py:55
  34.8 11.4 %fusion.27 = f32[2,192,768]{2,1,0:T(8,128)S(1)} fusion(f32[4096,768]{1,0:T(8,128)} %get-tuple-element.54, bf16[2,4096,192]{1,2,0:T(8,128)(2,1)} %copy-done.1, bf16[4096,192]{0,1:T(8,128)(2,1)S(1)} %copy-done.3, bf16[768,192]{0,1:T(8,128)(2,1)} %param.10), kind=kOutput, calls=%fused_computation.37 | convolution fusion | flops 4844421120 | bytes 18776064 | tf_op jit(solution)/shard_map/bd,tbf->tdf/dot_general | solution.py:24
  46.3 25.3 %psum.14 = s32[2]{0:T(128)S(1)} all-reduce(s32[2]{0:T(128)S(1)} %get-tuple-element.55), channel_id=1, replica_groups=mesh['data'=8] {'data'}, use_global_device_ids=true, to_apply=%region_3.0 | all-reduce | flops 2 | bytes 16 | tf_op jit(solution)/shard_map/psum | solution.py:50
  71.6 1.5 multiply_convert_fusion.5
  73.1 1.4 copy.21
  74.5 2.3 %all-to-all-start = ((bf16[2,8,18432]{2,0,1:T(2,128)(2,1)}), bf16[2,8,18432]{2,0,1:T(2,128)(2,1)S(1)}, u32[]{:S(2)}, u32[]{:S(2)}) async-start(bf16[2,8,18432]{2,0,1:T(2,128)(2,1)} %copy.21), calls=%async_computation | async-start | bytes 1179648 | tf_op jit(solution)/shard_map/all_to_all | solution.py:56
  76.8 1.4 copy.23
  78.2 9.0 %all-to-all-done = bf16[2,8,18432]{2,0,1:T(2,128)(2,1)S(1)} async-done(((bf16[2,8,18432]{2,0,1:T(2,128)(2,1)}), bf16[2,8,18432]{2,0,1:T(2,128)(2,1)S(1)}, u32[]{:S(2)}, u32[]{:S(2)}) %all-to-all-start) | async-done | bytes 589856 | tf_op jit(solution)/shard_map/all_to_all | solution.py:56
  87.2 2.3 %all-to-all-start.1 = ((bf16[2,8,18432]{2,0,1:T(2,128)(2,1)}), bf16[2,8,18432]{2,0,1:T(2,128)(2,1)S(1)}, u32[]{:S(2)}, u32[]{:S(2)}) async-start(bf16[2,8,18432]{2,0,1:T(2,128)(2,1)} %copy.23), calls=%async_computation.1 | async-start | bytes 1179648 | tf_op jit(solution)/shard_map/all_to_all | solution.py:56
  90.0 1.4 fusion.44
  91.4 8.4 %all-to-all-done.1 = bf16[2,8,18432]{2,0,1:T(2,128)(2,1)S(1)} async-done(((bf16[2,8,18432]{2,0,1:T(2,128)(2,1)}), bf16[2,8,18432]{2,0,1:T(2,128)(2,1)S(1)}, u32[]{:S(2)}, u32[]{:S(2)}) %all-to-all-start.1) | async-done | bytes 589856 | tf_op jit(solution)/shard_map/all_to_all | solution.py:56
  100.3 1.4 convolution_add_fusion.1
  101.8 22.2 %psum.15 = f32[2,2]{1,0:T(2,128)S(1)} all-reduce(f32[2,2]{1,0:T(2,128)S(1)} %convolution_add_fusion.1), channel_id=1, replica_groups=mesh['data'=8] {'data'}, use_global_device_ids=true, to_apply=%region_6.0 | all-reduce | flops 4 | bytes 32 | tf_op jit(solution)/shard_map/psum | solution.py:58
  125.3 28.4 %while.11 = (s32[]{:T(128)}, f32[2]{0:T(128)S(1)}, f32[2,2]{1,0:T(2,128)S(1)}, f32[]{:T(128)}, s32[]{:T(128)}, /*index=5*/s32[]{:T(128)}) while((s32[]{:T(128)}, f32[2]{0:T(128)S(1)}, f32[2,2]{1,0:T(2,128)S(1)}, f32[]{:T(128)}, s32[]{:T(128)}, /*index=5*/s32[]{:T(128)}) %tuple.33), condition=%wide.region_11.12_spmd.clone, body=%wide.region_8.11_spmd.clone.sunk | while | flops 22 | bytes 180 | solution.py:42
  125.4 0.6 fusion.57
  126.0 0.6 broadcast_divide_fusion.2
  126.8 0.6 fusion.57
  127.4 0.6 broadcast_divide_fusion.2
  128.9 0.6 broadcast_divide_fusion.2
  129.7 0.6 fusion.57
  130.3 0.6 broadcast_divide_fusion.2
  131.1 0.6 fusion.57
  131.7 0.6 broadcast_divide_fusion.2
  133.1 0.6 broadcast_divide_fusion.2
  133.9 0.6 fusion.57
  134.5 0.6 broadcast_divide_fusion.2
  135.3 0.6 fusion.57
  136.0 0.6 broadcast_divide_fusion.2
  137.4 0.6 broadcast_divide_fusion.2
  138.8 0.6 broadcast_divide_fusion.2
  140.2 0.6 broadcast_divide_fusion.2
  141.6 0.6 broadcast_divide_fusion.2
  143.1 0.6 broadcast_divide_fusion.2
  144.5 0.6 broadcast_divide_fusion.2
  145.9 0.6 broadcast_divide_fusion.2
  147.3 0.6 broadcast_divide_fusion.2
  148.7 0.6 broadcast_divide_fusion.2
  150.2 0.6 broadcast_divide_fusion.2
  151.6 0.6 broadcast_divide_fusion.2
  153.0 0.6 broadcast_divide_fusion.2
  153.7 1.1 multiply_reduce_fusion.1
  (75 shorter events, 12.9 us)
Async XLA Ops:
  0.6 1.0 copy-start
  1.6 13.2 %copy-start.2 = (bf16[4096,192]{0,1:T(8,128)(2,1)S(1)}, bf16[4096,192]{0,1:T(8,128)(2,1)}, u32[]{:S(2)}) copy-start(bf16[4096,192]{0,1:T(8,128)(2,1)} %param.8) | copy-start | bytes 4718596
  1.6 13.2 %copy-start.4 = (bf16[768,192]{0,1:T(8,128)(2,1)S(1)}, bf16[768,192]{0,1:T(8,128)(2,1)}, u32[]{:S(2)}) copy-start(bf16[768,192]{0,1:T(8,128)(2,1)} %param.10) | copy-start | bytes 884740
  1.6 13.2 %copy-start.7 = (bf16[2,192,10]{1,0,2:T(2,128)(2,1)S(1)}, bf16[2,192,10]{1,0,2:T(2,128)(2,1)}, u32[]{:S(2)}) copy-start(bf16[2,192,10]{1,0,2:T(2,128)(2,1)} %param.11) | copy-start | bytes 23044
  14.8 6.0 %copy-start.6 = (s32[2,4096]{1,0:T(2,128)S(1)}, s32[2,4096]{1,0:T(2,128)}, u32[]{:S(2)}) copy-start(s32[2,4096]{1,0:T(2,128)} %param.12) | copy-start | bytes 98308
  23.1 1.7 %copy-start.1 = (bf16[2,4096,192]{1,2,0:T(8,128)(2,1)}, bf16[2,4096,192]{1,2,0:T(8,128)(2,1)S(1)}, u32[]{:S(2)}) copy-start(bf16[2,4096,192]{1,2,0:T(8,128)(2,1)S(1)} %convolution_convert_fusion) | copy-start | bytes 9437188
  31.2 3.6 %copy-start.3 = (bf16[4096,192]{0,1:T(8,128)(2,1)S(1)}, bf16[4096,192]{0,1:T(8,128)(2,1)}, u32[]{:S(2)}) copy-start(bf16[4096,192]{0,1:T(8,128)(2,1)} %param.8) | copy-start | bytes 4718596
  74.5 12.7 %all-to-all-start = ((bf16[2,8,18432]{2,0,1:T(2,128)(2,1)}), bf16[2,8,18432]{2,0,1:T(2,128)(2,1)S(1)}, u32[]{:S(2)}, u32[]{:S(2)}) async-start(bf16[2,8,18432]{2,0,1:T(2,128)(2,1)} %copy.21), calls=%async_computation | async-start | bytes 1179648 | tf_op jit(solution)/shard_map/all_to_all | solution.py:56
  87.2 12.6 %all-to-all-start.1 = ((bf16[2,8,18432]{2,0,1:T(2,128)(2,1)}), bf16[2,8,18432]{2,0,1:T(2,128)(2,1)S(1)}, u32[]{:S(2)}, u32[]{:S(2)}) async-start(bf16[2,8,18432]{2,0,1:T(2,128)(2,1)} %copy.23), calls=%async_computation.1 | async-start | bytes 1179648 | tf_op jit(solution)/shard_map/all_to_all | solution.py:56
  153.7 1.1 copy-start.5
where the time goes:
time: 155 us
  blocking collectives  47.5 us (31%)
  matrix products  41.9 us (27%)
  other arithmetic  32.9 us (21%)
  waiting for transfers between devices  17.4 us (11%)
  local copies, waits for them, and re-layouts  8.3 us (5%)
  starting transfers between devices  4.55 us (3%)
    psum x1, blocking collectives, local_step(): label_count = lax.psum(mask_loc.sum(axis=1), 'data')  25.3 us
    psum x1, blocking collectives, local_step(): gram_mat = lax.psum(gram_of(shards[0]) + gram_of(shards[1]), 'data')  22.2 us
    all_to_all x2, waiting for transfers between devices, local_step(): arrived = lax.all_to_all(scaled, 'data', 1, 1, tiled=True)  17.4 us
    dot_general x1, matrix products, device_grads(): pre_act = jnp.dot(x_loc, w_in, preferred_element_type=jnp.float32)  13.2 us
    div x20, other arithmetic, solver_step(): return raised / raised.sum()  13 us
    reduce_sum x20, other arithmetic, solver_step(): return raised / raised.sum()  12.4 us
    dot_general x1, matrix products, device_grads(): jnp.einsum('bd,tbf->tdf', x_loc, d_pre, preferred_element_type=jnp.float32)  11.4 us
    dot_general x1, matrix products, device_grads(): jnp.einsum('bf,tbd->tfd', act_bf, d_resid, preferred_element_type=jnp.flo...  6.42 us
  transfers between devices with their start and end apart: 2, of which 2 were waited for; matrix products, arithmetic and copies ran while one was open for 2% of the time, Pallas kernels for 0%

commit v1 on v0

v1 whole, which is shorter than its diff:
```python
import functools

import jax
import jax.numpy as jnp
from jax import lax
from jax.experimental import pallas as pl
from jax.experimental.pallas import tpu as pltpu
from jax.sharding import PartitionSpec as P

SOLVER_STEPS = 20
MESH = pl.DeviceIdType.MESH
F32 = jnp.float32
BF16 = jnp.bfloat16
LANES = 128
SLOT = 16
C0 = 0.7978845608028654
C1 = 0.044715

NT = (((1,), (1,)), ((), ()))
TN = (((0,), (0,)), ((), ()))


def peer_of(me, k):
    y, x, c = me // 4, (me // 2) % 2, me % 2
    return ((y + k // 4) % 2) * 4 + ((x + (k // 2) % 2) % 2) * 2 + (c + k % 2) % 2


def kernel(n, tb, fc, x_ref, w1_ref, w2_ref, h_ref, lab_ref, mask_ref,
           alpha_ref, gin_ref, gout_ref,
           a_s, slope_s, dz_s, dzt_s, xt_s, q_s, w2t_s, hc_s, hbt_s,
           send2, recv2, send1, recv1, cnt_send, cnt_recv, m_send, m_recv,
           flat0, flat1, ta_s, tr_s,
           send_sem, recv_sem):
    me = lax.axis_index("data")
    tokens, model = x_ref.shape
    hidden = w1_ref.shape[1]
    classes = h_ref.shape[2]
    nblk, nchunk = tokens // tb, hidden // fc
    rows_in, rows_out = model // n, hidden // n

    barrier = pltpu.get_barrier_semaphore()
    for k in range(1, n):
        pl.semaphore_signal(barrier, inc=1, device_id=(peer_of(me, k),), device_id_type=MESH)

    cnt = jnp.zeros((2, LANES), F32)
    for b in range(tokens // LANES):
        cnt += mask_ref[:, b * LANES:(b + 1) * LANES].astype(F32)
    cnt_send[0:2, :] = cnt
    cnt_send[2:8, :] = jnp.zeros((6, LANES), F32)

    w2t_s[...] = w2_ref[...].T
    pad = jnp.zeros((model, LANES - classes), F32)
    h0 = jnp.concatenate([h_ref[0].astype(F32), pad], axis=1)
    h1 = jnp.concatenate([h_ref[1].astype(F32), pad], axis=1)
    h1 = pltpu.roll(h1, SLOT, 1)
    hc_s[...] = (h0 + h1).T[:2 * SLOT].astype(BF16)
    hbt = jnp.concatenate([h0[:LANES], h1[:LANES], h0[LANES:], h1[LANES:]], axis=0)
    hbt_s[...] = hbt[:, :2 * SLOT].astype(BF16)

    def copies(slot, src_of, dst):
        out = []
        for k in range(1, n):
            peer = peer_of(me, k)
            out.append(pltpu.make_async_remote_copy(
                src_ref=src_of(peer), dst_ref=dst, send_sem=send_sem.at[slot, k],
                recv_sem=recv_sem.at[slot, k], device_id=(peer,), device_id_type=MESH))
        return out

    cnt_copies = copies(0, lambda peer: cnt_send, cnt_recv.at[me])

    def forward(i, carry):
        tok = pl.ds(pl.multiple_of(i * tb, tb), tb)
        x_b = x_ref[tok, :]
        xt_s[:, tok] = x_b.T
        for c in range(nchunk):
            f = slice(c * fc, (c + 1) * fc)
            p = jnp.dot(x_b, w1_ref[:, f], preferred_element_type=F32)
            p2 = p * p
            t = jnp.tanh(p * (C0 + (C0 * C1) * p2))
            h = 0.5 + 0.5 * t
            a = p * h
            a_s[tok, f] = a.astype(BF16)
            slope_s[tok, f] = h + (a * (1.0 - h)) * (2 * C0 + (6 * C0 * C1) * p2)
        z = x_b.astype(F32) + jnp.dot(a_s[tok, :], w2_ref[...], preferred_element_type=F32)
        logits = lax.dot_general(hc_s[...], z.astype(BF16), NT, preferred_element_type=F32)
        e_all = []
        for t in range(2):
            lg = logits[t * SLOT:(t + 1) * SLOT]
            cls = lax.broadcasted_iota(jnp.int32, (SLOT, tb), 0)
            lg = jnp.where(cls < classes, lg, -jnp.inf)
            ex = jnp.exp(lg - lg.max(axis=0, keepdims=True))
            prob = ex * (1.0 / ex.sum(axis=0, keepdims=True))
            hot = (cls == lab_ref[t:t + 1, tok]).astype(F32)
            e = (mask_ref[t:t + 1, tok].astype(F32) * (prob - hot)).astype(BF16)
            e_all.append(e)
            dz_s[t, tok, :] = lax.dot_general(
                e, hc_s[t * SLOT:(t + 1) * SLOT, :], TN, preferred_element_type=F32).astype(BF16)
        e_cat = jnp.concatenate(e_all, axis=0)
        dzt_s[:, tok] = jnp.dot(hbt_s[...], e_cat, preferred_element_type=F32).astype(BF16)

        @pl.when(i == 1)
        def _():
            pl.semaphore_wait(barrier, n - 1)
            for c in cnt_copies:
                c.start()

        return carry

    lax.fori_loop(0, nblk, forward, 0)

    for c in cnt_copies:
        c.wait()
    cnt_recv[me] = cnt_send[...]
    tot = cnt_recv[0]
    for j in range(1, n):
        tot += cnt_recv[j]
    inv = 1.0 / jnp.maximum(tot.sum(axis=1, keepdims=True), 1.0)
    inv0, inv1 = inv[0:1], inv[1:2]

    for c in range(nchunk):
        f = slice(c * fc, (c + 1) * fc)
        d = jnp.dot(dzt_s[...], a_s[:, f], preferred_element_type=F32)
        tail = 2 * LANES + (model - LANES)
        d = jnp.concatenate([d[:LANES] * inv0, d[LANES:2 * LANES] * inv1,
                             d[2 * LANES:tail] * inv0, d[tail:] * inv1], axis=0)
        send2[f, :] = d.T.astype(BF16)

    def rows_of(peer):
        return send2.at[pl.ds(pl.multiple_of(peer * rows_out, rows_out), rows_out)]

    out_copies = copies(1, rows_of, recv2.at[me])
    for c in out_copies:
        c.start()

    in_copies = []
    for c in range(nchunk):
        f = slice(c * fc, (c + 1) * fc)

        def backward(i, carry):
            tok = pl.ds(pl.multiple_of(i * tb, tb), tb)
            sl = slope_s[tok, f]
            for t in range(2):
                da = jnp.dot(dz_s[t, tok, :], w2t_s[:, f], preferred_element_type=F32)
                q_s[t, tok, :] = (da * sl).astype(BF16)
            return carry

        lax.fori_loop(0, nblk, backward, 0)
        d0 = jnp.dot(xt_s[...], q_s[0], preferred_element_type=F32) * inv0
        d1 = jnp.dot(xt_s[...], q_s[1], preferred_element_type=F32) * inv1
        for j in range(n):
            r = slice(j * rows_in, (j + 1) * rows_in)
            send1[c, j] = jnp.concatenate([d0[r], d1[r]], axis=0).astype(BF16)
        now = copies(2 + c, lambda peer: send1.at[c, peer], recv1.at[c, me])
        for cp in now:
            cp.start()
        in_copies.append(now)

    for cp in out_copies:
        cp.wait()
    recv2[me] = send2[pl.ds(pl.multiple_of(me * rows_out, rows_out), rows_out), :]
    g2 = recv2[0].astype(F32)
    for j in range(1, n):
        g2 += recv2[j].astype(F32)
    t0, t1, r = g2[:, :LANES], g2[:, LANES:2 * LANES], g2[:, 2 * LANES:]
    r_sw = pltpu.roll(r, LANES // 2, 1)
    low = lax.broadcasted_iota(jnp.int32, (1, LANES), 1) < LANES // 2

    def fold(v):
        s = v[0:8]
        for b in range(1, v.shape[0] // 8):
            s += v[8 * b:8 * b + 8]
        return s

    zero = jnp.zeros((8, LANES), F32)
    rr = fold(r * r)
    m00 = fold(t0 * t0) + jnp.where(low, rr, zero)
    m11 = fold(t1 * t1) + jnp.where(low, zero, rr)
    m01 = fold(t0 * t1) + jnp.where(low, fold(r * r_sw), zero)

    half = rows_out // 2
    for t, flat in ((0, flat0), (1, flat1)):
        ta_s[...] = t0 if t == 0 else t1
        tr_s[...] = r if t == 0 else r_sw
        a_e, a_o = ta_s[pl.ds(0, half, stride=2), :], ta_s[pl.ds(1, half, stride=2), :]
        r_e, r_o = tr_s[pl.ds(0, half, stride=2), :], tr_s[pl.ds(1, half, stride=2), :]
        a_w = pltpu.roll(a_o, LANES // 2, 1)
        flat[1, pl.ds(0, half, stride=3), :] = a_e
        flat[1, pl.ds(1, half, stride=3), :] = jnp.where(low, r_e, a_w)
        flat[1, pl.ds(2, half, stride=3), :] = jnp.where(low, a_w, pltpu.roll(r_o, LANES // 2, 1))

    wide = hidden // LANES
    for c in range(nchunk):
        for cp in in_copies[c]:
            cp.wait()
        recv1[c, me] = send1[c, me]
        g1 = recv1[c, 0].astype(F32)
        for j in range(1, n):
            g1 += recv1[c, j].astype(F32)
        for b in range(fc // LANES):
            u = g1[:rows_in, b * LANES:(b + 1) * LANES]
            v = g1[rows_in:, b * LANES:(b + 1) * LANES]
            m00 += fold(u * u)
            m11 += fold(v * v)
            m01 += fold(u * v)
            flat0[0, pl.ds(c * (fc // LANES) + b, rows_in, stride=wide), :] = u
            flat1[0, pl.ds(c * (fc // LANES) + b, rows_in, stride=wide), :] = v

    row = lax.broadcasted_iota(jnp.int32, (8, LANES), 0)
    m_send[...] = jnp.where(row == 0, m00.sum(axis=0, keepdims=True),
                            jnp.where(row == 1, m01.sum(axis=0, keepdims=True),
                                      jnp.where(row == 2, m11.sum(axis=0, keepdims=True), zero)))
    m_copies = copies(2 + nchunk, lambda peer: m_send, m_recv.at[me])
    for cp in m_copies:
        cp.start()
    for cp in m_copies:
        cp.wait()
    m_recv[me] = m_send[...]
    gram = m_recv[0]
    for j in range(1, n):
        gram += m_recv[j]
    gram = jnp.broadcast_to(gram.sum(axis=1, keepdims=True), (8, LANES))
    g00, g01, g11 = gram[0:1], gram[1:2], gram[2:3]
    scale = 1.0 / ((g00 + g11) * 0.5)
    b0, b1 = (g00 - g01) * scale, (g01 - g11) * scale
    gap = jnp.zeros((1, LANES), F32)
    a0 = jnp.full((1, LANES), 0.5, F32)
    a1 = a0
    for _ in range(SOLVER_STEPS):
        gap = gap + (b0 * a0 + b1 * a1)
        ratio = jnp.exp(gap)
        a0 = 1.0 / (1.0 + ratio)
        a1 = ratio * a0
    lane = lax.broadcasted_iota(jnp.int32, (1, LANES), 1)
    alpha_ref[...] = jnp.where(lane == 0, a0, a1)
    gin_ref[...] = a0 * flat0[0] + a1 * flat1[0]
    gout_ref[...] = a0 * flat0[1] + a1 * flat1[1]


def solution(mesh):
    n = mesh.shape["data"]
    tb, fc = 512, 256

    def local_step(x_loc, w_in, w_out, task_heads, lab_loc, mask_loc):
        tokens, model = x_loc.shape
        hidden = w_in.shape[1]
        nchunk = hidden // fc
        piece = model * hidden // n // LANES
        rows_in, rows_out = model // n, hidden // n
        vmem = pl.BlockSpec(memory_space=pltpu.VMEM)
        alpha, g_in, g_out = pl.pallas_call(
            functools.partial(kernel, n, tb, fc),
            out_shape=(jax.ShapeDtypeStruct((1, LANES), F32),
                       jax.ShapeDtypeStruct((piece, LANES), F32),
                       jax.ShapeDtypeStruct((piece, LANES), F32)),
            in_specs=[vmem] * 6,
            out_specs=(vmem, vmem, vmem),
            scratch_shapes=[
                pltpu.VMEM((tokens, hidden), BF16),
                pltpu.VMEM((tokens, hidden), F32),
                pltpu.VMEM((2, tokens, model), BF16),
                pltpu.VMEM((2 * model, tokens), BF16),
                pltpu.VMEM((model, tokens), BF16),
                pltpu.VMEM((2, tokens, fc), BF16),
                pltpu.VMEM((model, hidden), BF16),
                pltpu.VMEM((2 * SLOT, model), BF16),
                pltpu.VMEM((2 * model, 2 * SLOT), BF16),
                pltpu.VMEM((hidden, 2 * model), BF16),
                pltpu.VMEM((n, rows_out, 2 * model), BF16),
                pltpu.VMEM((nchunk, n, 2 * rows_in, fc), BF16),
                pltpu.VMEM((nchunk, n, 2 * rows_in, fc), BF16),
                pltpu.VMEM((8, LANES), F32),
                pltpu.VMEM((n, 8, LANES), F32),
                pltpu.VMEM((8, LANES), F32),
                pltpu.VMEM((n, 8, LANES), F32),
                pltpu.VMEM((2, piece, LANES), F32),
                pltpu.VMEM((2, piece, LANES), F32),
                pltpu.VMEM((rows_out, LANES), F32),
                pltpu.VMEM((rows_out, LANES), F32),
                pltpu.SemaphoreType.DMA((3 + nchunk, n)),
                pltpu.SemaphoreType.DMA((3 + nchunk, n)),
            ],
            compiler_params=pltpu.CompilerParams(
                collective_id=0, has_side_effects=True, vmem_limit_bytes=60 * 1024 * 1024),
        )(x_loc, w_in, w_out, task_heads, lab_loc, mask_loc)
        return alpha[0, :2], g_in.reshape(-1), g_out.reshape(-1)

    return jax.shard_map(local_step, mesh=mesh, in_specs=(P("data", None), P(), P(), P(), P(None, "data"), P(None, "data")), out_specs=(P(), P("data"), P("data")), check_vma=False)
```

time: 155 us -> 52.9 us (0.34)
  blocking collectives: 47.5 us -> 0 us
  matrix products: 41.9 us -> 0 us
  Pallas kernels: 0 us -> 40.5 us
  other arithmetic: 32.9 us -> 0 us
  waiting for transfers between devices: 17.4 us -> 0 us
  starting transfers between devices: 4.55 us -> 0 us
  local copies, waits for them, and re-layouts: 8.3 us -> 11.4 us
    psum x2 -> x0, blocking collectives: 47.5 us -> none  [the longest x1 25.3 us: local_step(): label_count = lax.psum(mask_loc.sum(axis=1), 'data')]
    dot_general x7 -> x0, matrix products: 41.9 us -> none  [the longest x1 13.2 us: device_grads(): pre_act = jnp.dot(x_loc, w_in, preferred_element_type=jnp.float32)]
    pallas_call x0 -> x1, Pallas kernels: none -> 40.5 us  [local_step(): pl.pallas_call(functools.partial(kernel, n, tb, fc), out_shape=(jax.Shape...]
    reduce_sum x45 -> x0, other arithmetic: 18.4 us -> none  [the longest x20 12.4 us: solver_step(): return raised / raised.sum()]
    all_to_all x2 -> x0, waiting for transfers between devices: 17.4 us -> none  [local_step(): arrived = lax.all_to_all(scaled, 'data', 1, 1, tiled=True)]
    div x21 -> x0, other arithmetic: 13 us -> none  [the longest x20 13 us: solver_step(): return raised / raised.sum()]
    unnamed x16 -> x5, local copies, waits for them, and re-layouts: 1.72 us -> 10.3 us
    all_to_all x2 -> x0, starting transfers between devices: 4.55 us -> none  [local_step(): arrived = lax.all_to_all(scaled, 'data', 1, 1, tiled=True)]
  transfers between devices with their start and end apart: 2 -> 0, of which waited for: 2 -> 0; matrix products, arithmetic and copies ran while one was open for 2% -> 0% of each run, Pallas kernels for 0% -> 0%
where the time goes in v1:
time: 52.9 us; the launch traced here: 52.5 us
  Pallas kernels  40.5 us (77%)
  local copies, waits for them, and re-layouts  11.4 us (22%)
  between operations  0.64 us (1%)
    pallas_call x1, Pallas kernels, local_step(): pl.pallas_call(functools.partial(kernel, n, tb, fc), out_shape=(jax.Shape...  40.5 us
    unnamed x5, local copies, waits for them, and re-layouts  10.3 us
    squeeze x1, local copies, waits for them, and re-layouts, local_step(): return (alpha[0, :2], g_in.reshape(-1), g_out.reshape(-1))  1.12 us

profile of v1, /device:TPU:0, one launch (start us, length us, event | category | flops | bytes accessed | tf_op | source)
XLA Modules:
  0.0 52.5 jit_solution(16887463637896197805)
XLA Ops:
  0.6 1.5 %copy.11.h_ref = bf16[2,192,10]{2,1,0:T(8,128)(2,1)} copy(bf16[2,192,10]{1,0,2:T(2,128)(2,1)} %param.9) | data formatting | bytes 15360 | tf_op args[3]
  2.1 1.9 %copy.10.w2_ref = bf16[768,192]{1,0:T(8,128)(2,1)} copy(bf16[768,192]{0,1:T(8,128)(2,1)} %param.8) | data formatting | bytes 589824 | tf_op args[2]
  4.0 3.9 %copy.9.x_ref = bf16[4096,192]{1,0:T(8,128)(2,1)} copy(bf16[4096,192]{0,1:T(8,128)(2,1)} %param.6) | data formatting | bytes 3145728 | tf_op args[0]
  7.9 40.5 %shard_map.85 = (f32[1,128]{1,0:T(1,128)}, f32[144,128]{1,0:T(8,128)}, f32[144,128]{1,0:T(8,128)}) custom-call(bf16[4096,192]{1,0:T(8,128)(2,1)} %copy.9.x_ref, bf16[192,768]{1,0:T(8,128)(2,1)} %w1_ref.1, bf16[768,192]{1,0:T(8,128)(2,1)} %copy.10.w2_ref, bf16[2,192,10]{2,1,0:T(8,128)(2,1)} %copy.11.h_ref, s32[2,4096]{1,0:T(2,128)} %lab_ref.1, s32[2,4096]{1,0:T(2,128)} %mask_ref.1), custom_call_target="tpu_custom_call" | custom-call | tf_op jit(solution)/shard_map/pallas_call | solution.py:250
  48.4 1.1 %slice_bitcast_fusion = f32[2]{0:T(128)} fusion(f32[1,128]{1,0:T(1,128)} %get-tuple-element.6), kind=kLoop, calls=%fused_computation | loop fusion | bytes 16 | tf_op jit(solution)/shard_map/squeeze | solution.py:285
  49.5 1.5 %copy.14 = f32[18432]{0:T(1024)} copy(f32[18432]{0:T(1024)} %bitcast.5) | data formatting | bytes 147456
  51.0 1.5 %copy.15 = f32[18432]{0:T(1024)} copy(f32[18432]{0:T(1024)} %bitcast.4) | data formatting | bytes 147456

commit v2 on v1

--- a/solution.py
+++ b/solution.py
@@ -25,16 +25,16 @@
     return ((y + k // 4) % 2) * 4 + ((x + (k // 2) % 2) % 2) * 2 + (c + k % 2) % 2
 
 
-def kernel(n, tb, fc, x_ref, w1_ref, w2_ref, h_ref, lab_ref, mask_ref,
-           alpha_ref, gin_ref, gout_ref,
-           a_s, slope_s, dz_s, dzt_s, xt_s, q_s, w2t_s, hc_s, hbt_s,
+def kernel(n, tb, fc, xt_ref, w1_ref, w2t_ref, h_ref, lab_ref, mask_ref,
+           flat0, flat1, gram_ref,
+           a_s, slope_s, dz_s, dzt_s, z_s, q_s, w2_s, hc_s, hbt_s,
            send2, recv2, send1, recv1, cnt_send, cnt_recv, m_send, m_recv,
-           flat0, flat1, ta_s, tr_s,
+           ta_s, tr_s,
            send_sem, recv_sem):
     me = lax.axis_index("data")
-    tokens, model = x_ref.shape
+    model, tokens = xt_ref.shape
     hidden = w1_ref.shape[1]
-    classes = h_ref.shape[2]
+    classes = h_ref.shape[0]
     nblk, nchunk = tokens // tb, hidden // fc
     rows_in, rows_out = model // n, hidden // n
 
@@ -48,12 +48,15 @@
     cnt_send[0:2, :] = cnt
     cnt_send[2:8, :] = jnp.zeros((6, LANES), F32)
 
-    w2t_s[...] = w2_ref[...].T
-    pad = jnp.zeros((model, LANES - classes), F32)
-    h0 = jnp.concatenate([h_ref[0].astype(F32), pad], axis=1)
-    h1 = jnp.concatenate([h_ref[1].astype(F32), pad], axis=1)
-    h1 = pltpu.roll(h1, SLOT, 1)
-    hc_s[...] = (h0 + h1).T[:2 * SLOT].astype(BF16)
+    w2_s[...] = w2t_ref[...].T
+    heads = h_ref[...].astype(F32)
+    gap = jnp.zeros((SLOT - classes, model), F32)
+    hc = jnp.concatenate([heads[:, 0], gap, heads[:, 1], gap], axis=0)
+    hc_s[...] = hc.astype(BF16)
+    full = jnp.concatenate([hc, jnp.zeros((LANES - 2 * SLOT, model), F32)], axis=0).T
+    lane = lax.broadcasted_iota(jnp.int32, (1, LANES), 1)
+    h0 = jnp.where(lane < SLOT, full, 0.0)
+    h1 = jnp.where(lane < SLOT, 0.0, full)
     hbt = jnp.concatenate([h0[:LANES], h1[:LANES], h0[LANES:], h1[LANES:]], axis=0)
     hbt_s[...] = hbt[:, :2 * SLOT].astype(BF16)
 
@@ -68,21 +71,12 @@
 
     cnt_copies = copies(0, lambda peer: cnt_send, cnt_recv.at[me])
 
-    def forward(i, carry):
-        tok = pl.ds(pl.multiple_of(i * tb, tb), tb)
-        x_b = x_ref[tok, :]
-        xt_s[:, tok] = x_b.T
-        for c in range(nchunk):
-            f = slice(c * fc, (c + 1) * fc)
-            p = jnp.dot(x_b, w1_ref[:, f], preferred_element_type=F32)
-            p2 = p * p
-            t = jnp.tanh(p * (C0 + (C0 * C1) * p2))
-            h = 0.5 + 0.5 * t
-            a = p * h
-            a_s[tok, f] = a.astype(BF16)
-            slope_s[tok, f] = h + (a * (1.0 - h)) * (2 * C0 + (6 * C0 * C1) * p2)
-        z = x_b.astype(F32) + jnp.dot(a_s[tok, :], w2_ref[...], preferred_element_type=F32)
-        logits = lax.dot_general(hc_s[...], z.astype(BF16), NT, preferred_element_type=F32)
+    def block(i):
+        return pl.ds(pl.multiple_of(i * tb, tb), tb)
+
+    def errors(i, slot):
+        tok = block(i)
+        logits = lax.dot_general(hc_s[...], z_s[slot], NT, preferred_element_type=F32)
         e_all = []
         for t in range(2):
             lg = logits[t * SLOT:(t + 1) * SLOT]
@@ -98,6 +92,27 @@
         e_cat = jnp.concatenate(e_all, axis=0)
         dzt_s[:, tok] = jnp.dot(hbt_s[...], e_cat, preferred_element_type=F32).astype(BF16)
 
+    def trunk(i, slot):
+        tok = block(i)
+        x_b = xt_ref[:, tok].T
+        for c in range(nchunk):
+            f = slice(c * fc, (c + 1) * fc)
+            p = jnp.dot(x_b, w1_ref[:, f], preferred_element_type=F32)
+            p2 = p * p
+            t = jnp.tanh(p * (C0 + (C0 * C1) * p2))
+            h = 0.5 + 0.5 * t
+            a = p * h
+            a_s[tok, f] = a.astype(BF16)
+            slope_s[tok, f] = h + (a * (1.0 - h)) * (2 * C0 + (6 * C0 * C1) * p2)
+        z = x_b.astype(F32) + jnp.dot(a_s[tok, :], w2_s[...], preferred_element_type=F32)
+        z_s[slot] = z.astype(BF16)
+
+    trunk(0, 0)
+
+    def forward(i, carry):
+        errors(i - 1, (i - 1) % 2)
+        trunk(i, i % 2)
+
         @pl.when(i == 1)
         def _():
             pl.semaphore_wait(barrier, n - 1)
@@ -106,7 +121,8 @@
 
         return carry
 
-    lax.fori_loop(0, nblk, forward, 0)
+    lax.fori_loop(1, nblk, forward, 0)
+    errors(nblk - 1, (nblk - 1) % 2)
 
     for c in cnt_copies:
         c.wait()
@@ -136,17 +152,14 @@
     for c in range(nchunk):
         f = slice(c * fc, (c + 1) * fc)
 
-        def backward(i, carry):
-            tok = pl.ds(pl.multiple_of(i * tb, tb), tb)
+        for i in range(nblk):
+            tok = slice(i * tb, (i + 1) * tb)
             sl = slope_s[tok, f]
             for t in range(2):
-                da = jnp.dot(dz_s[t, tok, :], w2t_s[:, f], preferred_element_type=F32)
+                da = jnp.dot(dz_s[t, tok, :], w2t_ref[:, f], preferred_element_type=F32)
                 q_s[t, tok, :] = (da * sl).astype(BF16)
-            return carry
-
-        lax.fori_loop(0, nblk, backward, 0)
-        d0 = jnp.dot(xt_s[...], q_s[0], preferred_element_type=F32) * inv0
-        d1 = jnp.dot(xt_s[...], q_s[1], preferred_element_type=F32) * inv1
+        d0 = jnp.dot(xt_ref[...], q_s[0], preferred_element_type=F32) * inv0
+        d1 = jnp.dot(xt_ref[...], q_s[1], preferred_element_type=F32) * inv1
         for j in range(n):
             r = slice(j * rows_in, (j + 1) * rows_in)
             send1[c, j] = jnp.concatenate([d0[r], d1[r]], axis=0).astype(BF16)
@@ -218,7 +231,11 @@
     gram = m_recv[0]
     for j in range(1, n):
         gram += m_recv[j]
-    gram = jnp.broadcast_to(gram.sum(axis=1, keepdims=True), (8, LANES))
+    gram_ref[...] = gram
+
+
+def finish(u0_ref, u1_ref, gram_ref, alpha_ref, gin_ref, gout_ref):
+    gram = jnp.broadcast_to(gram_ref[...].sum(axis=1, keepdims=True), (8, LANES))
     g00, g01, g11 = gram[0:1], gram[1:2], gram[2:3]
     scale = 1.0 / ((g00 + g11) * 0.5)
     b0, b1 = (g00 - g01) * scale, (g01 - g11) * scale
@@ -230,10 +247,10 @@
         ratio = jnp.exp(gap)
         a0 = 1.0 / (1.0 + ratio)
         a1 = ratio * a0
-    lane = lax.broadcasted_iota(jnp.int32, (1, LANES), 1)
-    alpha_ref[...] = jnp.where(lane == 0, a0, a1)
-    gin_ref[...] = a0 * flat0[0] + a1 * flat1[0]
-    gout_ref[...] = a0 * flat0[1] + a1 * flat1[1]
+    alpha_ref[0] = a0[0, 0]
+    alpha_ref[1] = a1[0, 0]
+    gin_ref[...] = a0 * u0_ref[0] + a1 * u1_ref[0]
+    gout_ref[...] = a0 * u0_ref[1] + a1 * u1_ref[1]
 
 
 def solution(mesh):
@@ -247,11 +264,11 @@
         piece = model * hidden // n // LANES
         rows_in, rows_out = model // n, hidden // n
         vmem = pl.BlockSpec(memory_space=pltpu.VMEM)
-        alpha, g_in, g_out = pl.pallas_call(
+        u0, u1, gram = pl.pallas_call(
             functools.partial(kernel, n, tb, fc),
-            out_shape=(jax.ShapeDtypeStruct((1, LANES), F32),
-                       jax.ShapeDtypeStruct((piece, LANES), F32),
-                       jax.ShapeDtypeStruct((piece, LANES), F32)),
+            out_shape=(jax.ShapeDtypeStruct((2, piece, LANES), F32),
+                       jax.ShapeDtypeStruct((2, piece, LANES), F32),
+                       jax.ShapeDtypeStruct((8, LANES), F32)),
             in_specs=[vmem] * 6,
             out_specs=(vmem, vmem, vmem),
             scratch_shapes=[
@@ -259,9 +276,9 @@
                 pltpu.VMEM((tokens, hidden), F32),
                 pltpu.VMEM((2, tokens, model), BF16),
                 pltpu.VMEM((2 * model, tokens), BF16),
-                pltpu.VMEM((model, tokens), BF16),
+                pltpu.VMEM((2, tb, model), BF16),
                 pltpu.VMEM((2, tokens, fc), BF16),
-                pltpu.VMEM((model, hidden), BF16),
+                pltpu.VMEM((hidden, model), BF16),
                 pltpu.VMEM((2 * SLOT, model), BF16),
                 pltpu.VMEM((2 * model, 2 * SLOT), BF16),
                 pltpu.VMEM((hidden, 2 * model), BF16),
@@ -272,8 +289,6 @@
                 pltpu.VMEM((n, 8, LANES), F32),
                 pltpu.VMEM((8, LANES), F32),
                 pltpu.VMEM((n, 8, LANES), F32),
-                pltpu.VMEM((2, piece, LANES), F32),
-                pltpu.VMEM((2, piece, LANES), F32),
                 pltpu.VMEM((rows_out, LANES), F32),
                 pltpu.VMEM((rows_out, LANES), F32),
                 pltpu.SemaphoreType.DMA((3 + nchunk, n)),
@@ -281,7 +296,15 @@
             ],
             compiler_params=pltpu.CompilerParams(
                 collective_id=0, has_side_effects=True, vmem_limit_bytes=60 * 1024 * 1024),
-        )(x_loc, w_in, w_out, task_heads, lab_loc, mask_loc)
-        return alpha[0, :2], g_in.reshape(-1), g_out.reshape(-1)
+        )(x_loc.T, w_in, w_out.T, jnp.transpose(task_heads, (2, 0, 1)), lab_loc, mask_loc)
+        alpha, g_in, g_out = pl.pallas_call(
+            finish,
+            out_shape=(jax.ShapeDtypeStruct((2,), F32),
+                       jax.ShapeDtypeStruct((piece, LANES), F32),
+                       jax.ShapeDtypeStruct((piece, LANES), F32)),
+            in_specs=[vmem] * 3,
+            out_specs=(pl.BlockSpec(memory_space=pltpu.SMEM), vmem, vmem),
+        )(u0, u1, gram)
+        return alpha, g_in.reshape(-1), g_out.reshape(-1)
 
     return jax.shard_map(local_step, mesh=mesh, in_specs=(P("data", None), P(), P(), P(), P(None, "data"), P(None, "data")), out_specs=(P(), P("data"), P("data")), check_vma=False)

time: 52.9 us -> 42.6 us (0.81)
  local copies, waits for them, and re-layouts: 11.4 us -> 0 us
  Pallas kernels: 40.5 us -> 41.8 us
    unnamed x5 -> x0, local copies, waits for them, and re-layouts: 10.3 us -> none
    pallas_call x0 -> x1, Pallas kernels: none -> 2.15 us  [local_step(): pl.pallas_call(finish, out_shape=(jax.ShapeDtypeStruct((2,), F32), jax.Sh...]
    squeeze x1 -> x0, local copies, waits for them, and re-layouts: 1.12 us -> none  [local_step(): return (alpha[0, :2], g_in.reshape(-1), g_out.reshape(-1))]
    pallas_call x1, Pallas kernels: 40.5 us -> 39.7 us  [local_step(): pl.pallas_call(functools.partial(kernel, n, tb, fc), out_shape=(jax.Shape...]
where the time goes in v2:
time: 42.6 us; the launch traced here: 42.4 us
  Pallas kernels  41.8 us (98%)
  between operations  0.64 us (2%)
    pallas_call x1, Pallas kernels, local_step(): pl.pallas_call(functools.partial(kernel, n, tb, fc), out_shape=(jax.Shape...  39.7 us
    pallas_call x1, Pallas kernels, local_step(): pl.pallas_call(finish, out_shape=(jax.ShapeDtypeStruct((2,), F32), jax.Sh...  2.15 us

profile of v2, /device:TPU:0, one launch (start us, length us, event | category | flops | bytes accessed | tf_op | source)
XLA Modules:
  0.0 42.4 jit_solution(9042447610716445919)
XLA Ops:
  0.6 39.7 %shard_map.85 = (f32[2,144,128]{2,1,0:T(8,128)}, f32[2,144,128]{2,1,0:T(8,128)}, f32[8,128]{1,0:T(8,128)}) custom-call(bf16[192,4096]{1,0:T(8,128)(2,1)} %bitcast.5, bf16[192,768]{1,0:T(8,128)(2,1)} %w1_ref.1, bf16[192,768]{1,0:T(8,128)(2,1)} %bitcast.6, bf16[10,2,192]{2,1,0:T(2,128)(2,1)} %bitcast.7, s32[2,4096]{1,0:T(2,128)} %lab_ref.1, s32[2,4096]{1,0:T(2,128)} %mask_ref.1), custom_call_target="tpu_custom_call" | custom-call | tf_op jit(solution)/shard_map/pallas_call | solution.py:267
  40.3 2.1 %shard_map.86 = (f32[2]{0:T(128)}, f32[144,128]{1,0:T(8,128)}, f32[144,128]{1,0:T(8,128)}) custom-call(f32[2,144,128]{2,1,0:T(8,128)} %get-tuple-element.9.u0_ref, f32[2,144,128]{2,1,0:T(8,128)} %get-tuple-element.10.u1_ref, f32[8,128]{1,0:T(8,128)} %get-tuple-element.11.gram_ref), custom_call_target="tpu_custom_call" | custom-call | tf_op jit(solution)/shard_map/pallas_call | solution.py:300

commit v3 on v2

--- a/solution.py
+++ b/solution.py
@@ -25,9 +25,9 @@
     return ((y + k // 4) % 2) * 4 + ((x + (k // 2) % 2) % 2) * 2 + (c + k % 2) % 2
 
 
-def kernel(n, tb, fc, xt_ref, w1_ref, w2t_ref, h_ref, lab_ref, mask_ref,
+def kernel(n, tb, rp, fc, xt_ref, w1_ref, w2t_ref, h_ref, lab_ref, mask_ref,
            flat0, flat1, gram_ref,
-           a_s, slope_s, dz_s, dzt_s, z_s, q_s, w2_s, hc_s, hbt_s,
+           x_s, sl_s, a_s, p_s, e_s, dz_s, dzt_s, z_s, acc_s, q_s, w2_s, hc_s, hbt_s,
            send2, recv2, send1, recv1, cnt_send, cnt_recv, m_send, m_recv,
            ta_s, tr_s,
            send_sem, recv_sem):
@@ -72,12 +72,36 @@
     cnt_copies = copies(0, lambda peer: cnt_send, cnt_recv.at[me])
 
     def block(i):
-        return pl.ds(pl.multiple_of(i * tb, tb), tb)
-
-    def errors(i, slot):
+        return slice(i * tb, (i + 1) * tb)
+
+    def chunk(c):
+        return pl.ds(pl.multiple_of(c * fc, fc), fc) if not isinstance(c, int) else slice(c * fc, (c + 1) * fc)
+
+    def enter(i):
+        if i < nblk:
+            x_s[block(i), :] = xt_ref[:, block(i)].T
+
+    def project(i, c):
+        if i < nblk:
+            p_s[block(i), chunk(c)] = jnp.dot(x_s[block(i), :], w1_ref[:, chunk(c)], preferred_element_type=F32)
+
+    def activate(i, c):
+        if i < nblk:
+            p = p_s[block(i), chunk(c)]
+            t = jnp.tanh(p * (C0 + (C0 * C1) * (p * p)))
+            a_s[block(i), chunk(c)] = (p * (0.5 + 0.5 * t)).astype(BF16)
+
+    def residual(i):
+        if 0 <= i < nblk:
+            tok = block(i)
+            z = x_s[tok, :].astype(F32) + jnp.dot(a_s[tok, :], w2_s[...], preferred_element_type=F32)
+            z_s[tok, :] = z.astype(BF16)
+
+    def errors(i):
+        if not 0 <= i < nblk:
+            return
         tok = block(i)
-        logits = lax.dot_general(hc_s[...], z_s[slot], NT, preferred_element_type=F32)
-        e_all = []
+        logits = lax.dot_general(hc_s[...], z_s[tok, :], NT, preferred_element_type=F32)
         for t in range(2):
             lg = logits[t * SLOT:(t + 1) * SLOT]
             cls = lax.broadcasted_iota(jnp.int32, (SLOT, tb), 0)
@@ -85,44 +109,36 @@
             ex = jnp.exp(lg - lg.max(axis=0, keepdims=True))
             prob = ex * (1.0 / ex.sum(axis=0, keepdims=True))
             hot = (cls == lab_ref[t:t + 1, tok]).astype(F32)
-            e = (mask_ref[t:t + 1, tok].astype(F32) * (prob - hot)).astype(BF16)
-            e_all.append(e)
-            dz_s[t, tok, :] = lax.dot_general(
-                e, hc_s[t * SLOT:(t + 1) * SLOT, :], TN, preferred_element_type=F32).astype(BF16)
-        e_cat = jnp.concatenate(e_all, axis=0)
-        dzt_s[:, tok] = jnp.dot(hbt_s[...], e_cat, preferred_element_type=F32).astype(BF16)
-
-    def trunk(i, slot):
-        tok = block(i)
-        x_b = xt_ref[:, tok].T
+            e = mask_ref[t:t + 1, tok].astype(F32) * (prob - hot)
+            e_s[t * SLOT:(t + 1) * SLOT, tok] = e.astype(BF16)
+
+    def back_t(i):
+        if 0 <= i < nblk:
+            tok = block(i)
+            dzt_s[:, tok] = jnp.dot(hbt_s[...], e_s[:, tok], preferred_element_type=F32).astype(BF16)
+
+    enter(0)
+    for c in range(nchunk):
+        project(0, c)
+    enter(1)
+    for i in range(nblk + 2):
+        enter(i + 2)
+        residual(i - 1)
         for c in range(nchunk):
-            f = slice(c * fc, (c + 1) * fc)
-            p = jnp.dot(x_b, w1_ref[:, f], preferred_element_type=F32)
-            p2 = p * p
-            t = jnp.tanh(p * (C0 + (C0 * C1) * p2))
-            h = 0.5 + 0.5 * t
-            a = p * h
-            a_s[tok, f] = a.astype(BF16)
-            slope_s[tok, f] = h + (a * (1.0 - h)) * (2 * C0 + (6 * C0 * C1) * p2)
-        z = x_b.astype(F32) + jnp.dot(a_s[tok, :], w2_s[...], preferred_element_type=F32)
-        z_s[slot] = z.astype(BF16)
-
-    trunk(0, 0)
-
-    def forward(i, carry):
-        errors(i - 1, (i - 1) % 2)
-        trunk(i, i % 2)
-
-        @pl.when(i == 1)
-        def _():
+            activate(i, c)
+            project(i + 1, c)
+        errors(i - 1)
+        back_t(i - 2)
+        if i == nblk // 2 + 1:
             pl.semaphore_wait(barrier, n - 1)
             for c in cnt_copies:
                 c.start()
 
+    def w2_part(c, carry):
+        acc_s[:, chunk(c)] = jnp.dot(dzt_s[...], a_s[:, chunk(c)], preferred_element_type=F32)
         return carry
 
-    lax.fori_loop(1, nblk, forward, 0)
-    errors(nblk - 1, (nblk - 1) % 2)
+    lax.fori_loop(0, nchunk, w2_part, 0)
 
     for c in cnt_copies:
         c.wait()
@@ -135,7 +151,7 @@
 
     for c in range(nchunk):
         f = slice(c * fc, (c + 1) * fc)
-        d = jnp.dot(dzt_s[...], a_s[:, f], preferred_element_type=F32)
+        d = acc_s[:, f]
         tail = 2 * LANES + (model - LANES)
         d = jnp.concatenate([d[:LANES] * inv0, d[LANES:2 * LANES] * inv1,
                              d[2 * LANES:tail] * inv0, d[tail:] * inv1], axis=0)
@@ -148,25 +164,44 @@
     for c in out_copies:
         c.start()
 
-    in_copies = []
-    for c in range(nchunk):
-        f = slice(c * fc, (c + 1) * fc)
-
+    def copies_in(c):
+        return copies(2 + c, lambda peer: send1.at[c, peer], recv1.at[c, me])
+
+    def back(i, carry):
+        tok = pl.ds(pl.multiple_of(i * 2 * tb, 2 * tb), 2 * tb)
+        for t in range(2):
+            row = slice(t * SLOT, (t + 1) * SLOT)
+            dz_s[t, tok, :] = lax.dot_general(
+                e_s[row, tok], hc_s[row, :], TN, preferred_element_type=F32).astype(BF16)
+        return carry
+
+    lax.fori_loop(0, nblk // 2, back, 0)
+
+    def w1_part(c, carry):
         for i in range(nblk):
-            tok = slice(i * tb, (i + 1) * tb)
-            sl = slope_s[tok, f]
             for t in range(2):
-                da = jnp.dot(dz_s[t, tok, :], w2t_ref[:, f], preferred_element_type=F32)
-                q_s[t, tok, :] = (da * sl).astype(BF16)
+                da = jnp.dot(dz_s[t, block(i), :], w2t_ref[:, chunk(c)], preferred_element_type=F32)
+                for r in range(0, tb, rp):
+                    rows = slice(i * tb + r, i * tb + r + rp)
+                    if t == 0:
+                        p = p_s[rows, chunk(c)]
+                        p2 = p * p
+                        h = 0.5 + 0.5 * jnp.tanh(p * (C0 + (C0 * C1) * p2))
+                        sl = h + (p * h * (1.0 - h)) * (2 * C0 + (6 * C0 * C1) * p2)
+                        sl_s[r:r + rp, :] = sl
+                    else:
+                        sl = sl_s[r:r + rp, :]
+                    q_s[t, rows, :] = (da[r:r + rp] * sl).astype(BF16)
         d0 = jnp.dot(xt_ref[...], q_s[0], preferred_element_type=F32) * inv0
         d1 = jnp.dot(xt_ref[...], q_s[1], preferred_element_type=F32) * inv1
         for j in range(n):
             r = slice(j * rows_in, (j + 1) * rows_in)
             send1[c, j] = jnp.concatenate([d0[r], d1[r]], axis=0).astype(BF16)
-        now = copies(2 + c, lambda peer: send1.at[c, peer], recv1.at[c, me])
-        for cp in now:
+        for cp in copies_in(c):
             cp.start()
-        in_copies.append(now)
+        return carry
+
+    lax.fori_loop(0, nchunk, w1_part, 0)
 
     for cp in out_copies:
         cp.wait()
@@ -190,20 +225,20 @@
     m11 = fold(t1 * t1) + jnp.where(low, zero, rr)
     m01 = fold(t0 * t1) + jnp.where(low, fold(r * r_sw), zero)
 
-    half = rows_out // 2
+    pairs = rows_out // 2
     for t, flat in ((0, flat0), (1, flat1)):
         ta_s[...] = t0 if t == 0 else t1
         tr_s[...] = r if t == 0 else r_sw
-        a_e, a_o = ta_s[pl.ds(0, half, stride=2), :], ta_s[pl.ds(1, half, stride=2), :]
-        r_e, r_o = tr_s[pl.ds(0, half, stride=2), :], tr_s[pl.ds(1, half, stride=2), :]
+        a_e, a_o = ta_s[pl.ds(0, pairs, stride=2), :], ta_s[pl.ds(1, pairs, stride=2), :]
+        r_e, r_o = tr_s[pl.ds(0, pairs, stride=2), :], tr_s[pl.ds(1, pairs, stride=2), :]
         a_w = pltpu.roll(a_o, LANES // 2, 1)
-        flat[1, pl.ds(0, half, stride=3), :] = a_e
-        flat[1, pl.ds(1, half, stride=3), :] = jnp.where(low, r_e, a_w)
-        flat[1, pl.ds(2, half, stride=3), :] = jnp.where(low, a_w, pltpu.roll(r_o, LANES // 2, 1))
+        flat[1, pl.ds(0, pairs, stride=3), :] = a_e
+        flat[1, pl.ds(1, pairs, stride=3), :] = jnp.where(low, r_e, a_w)
+        flat[1, pl.ds(2, pairs, stride=3), :] = jnp.where(low, a_w, pltpu.roll(r_o, LANES // 2, 1))
 
     wide = hidden // LANES
     for c in range(nchunk):
-        for cp in in_copies[c]:
+        for cp in copies_in(c):
             cp.wait()
         recv1[c, me] = send1[c, me]
         g1 = recv1[c, 0].astype(F32)
@@ -255,7 +290,7 @@
 
 def solution(mesh):
     n = mesh.shape["data"]
-    tb, fc = 512, 256
+    tb, rp, fc = 512, 64, 256
 
     def local_step(x_loc, w_in, w_out, task_heads, lab_loc, mask_loc):
         tokens, model = x_loc.shape
@@ -265,18 +300,22 @@
         rows_in, rows_out = model // n, hidden // n
         vmem = pl.BlockSpec(memory_space=pltpu.VMEM)
         u0, u1, gram = pl.pallas_call(
-            functools.partial(kernel, n, tb, fc),
+            functools.partial(kernel, n, tb, rp, fc),
             out_shape=(jax.ShapeDtypeStruct((2, piece, LANES), F32),
                        jax.ShapeDtypeStruct((2, piece, LANES), F32),
                        jax.ShapeDtypeStruct((8, LANES), F32)),
             in_specs=[vmem] * 6,
             out_specs=(vmem, vmem, vmem),
             scratch_shapes=[
+                pltpu.VMEM((tokens, model), BF16),
+                pltpu.VMEM((tb, fc), F32),
                 pltpu.VMEM((tokens, hidden), BF16),
                 pltpu.VMEM((tokens, hidden), F32),
+                pltpu.VMEM((2 * SLOT, tokens), BF16),
                 pltpu.VMEM((2, tokens, model), BF16),
                 pltpu.VMEM((2 * model, tokens), BF16),
-                pltpu.VMEM((2, tb, model), BF16),
+                pltpu.VMEM((tokens, model), BF16),
+                pltpu.VMEM((2 * model, hidden), F32),
                 pltpu.VMEM((2, tokens, fc), BF16),
                 pltpu.VMEM((hidden, model), BF16),
                 pltpu.VMEM((2 * SLOT, model), BF16),
@@ -295,7 +334,7 @@
                 pltpu.SemaphoreType.DMA((3 + nchunk, n)),
             ],
             compiler_params=pltpu.CompilerParams(
-                collective_id=0, has_side_effects=True, vmem_limit_bytes=60 * 1024 * 1024),
+                collective_id=0, has_side_effects=True, vmem_limit_bytes=65000 * 1024),
         )(x_loc.T, w_in, w_out.T, jnp.transpose(task_heads, (2, 0, 1)), lab_loc, mask_loc)
         alpha, g_in, g_out = pl.pallas_call(
             finish,

time: 42.6 us -> 37.5 us (0.88)
  Pallas kernels: 41.8 us -> 36.7 us
    pallas_call x1, Pallas kernels: 39.7 us -> 34.6 us  [local_step(): pl.pallas_call(functools.partial(kernel, n, tb, rp, fc), out_shape=(jax.S...]
where the time goes in v3:
time: 37.5 us; the launch traced here: 37.4 us
  Pallas kernels  36.7 us (98%)
  between operations  0.64 us (2%)
    pallas_call x1, Pallas kernels, local_step(): pl.pallas_call(functools.partial(kernel, n, tb, rp, fc), out_shape=(jax.S...  34.6 us
    pallas_call x1, Pallas kernels, local_step(): pl.pallas_call(finish, out_shape=(jax.ShapeDtypeStruct((2,), F32), jax.Sh...  2.15 us

profile of v3, /device:TPU:0, one launch (start us, length us, event | category | flops | bytes accessed | tf_op | source)
XLA Modules:
  0.0 37.4 jit_solution(6311936902917777271)
XLA Ops:
  0.6 34.6 %shard_map.85 = (f32[2,144,128]{2,1,0:T(8,128)}, f32[2,144,128]{2,1,0:T(8,128)}, f32[8,128]{1,0:T(8,128)}) custom-call(bf16[192,4096]{1,0:T(8,128)(2,1)} %bitcast.5, bf16[192,768]{1,0:T(8,128)(2,1)} %w1_ref.1, bf16[192,768]{1,0:T(8,128)(2,1)} %bitcast.6, bf16[10,2,192]{2,1,0:T(2,128)(2,1)} %bitcast.7, s32[2,4096]{1,0:T(2,128)} %lab_ref.1, s32[2,4096]{1,0:T(2,128)} %mask_ref.1), custom_call_target="tpu_custom_call" | custom-call | tf_op jit(solution)/shard_map/pallas_call | solution.py:302
  35.2 2.1 %shard_map.86 = (f32[2]{0:T(128)}, f32[144,128]{1,0:T(8,128)}, f32[144,128]{1,0:T(8,128)}) custom-call(f32[2,144,128]{2,1,0:T(8,128)} %get-tuple-element.9.u0_ref, f32[2,144,128]{2,1,0:T(8,128)} %get-tuple-element.10.u1_ref, f32[8,128]{1,0:T(8,128)} %get-tuple-element.11.gram_ref), custom_call_target="tpu_custom_call" | custom-call | tf_op jit(solution)/shard_map/pallas_call | solution.py:339

commit v4 on v3

--- a/solution.py
+++ b/solution.py
@@ -27,7 +27,7 @@
 
 def kernel(n, tb, rp, fc, xt_ref, w1_ref, w2t_ref, h_ref, lab_ref, mask_ref,
            flat0, flat1, gram_ref,
-           x_s, sl_s, a_s, p_s, e_s, dz_s, dzt_s, z_s, acc_s, q_s, w2_s, hc_s, hbt_s,
+           x_s, sl_s, a_s, p_s, e_s, dz_s, dzt_s, z_s, acc_s, inv_s, w1h_s, w2h_s, q_s, w2_s, hc_s, hbt_s,
            send2, recv2, send1, recv1, cnt_send, cnt_recv, m_send, m_recv,
            ta_s, tr_s,
            send_sem, recv_sem):
@@ -49,6 +49,8 @@
     cnt_send[2:8, :] = jnp.zeros((6, LANES), F32)
 
     w2_s[...] = w2t_ref[...].T
+    w1h_s[...] = (w1_ref[...].astype(F32) * 0.5).astype(BF16)
+    w2h_s[...] = (w2t_ref[...].astype(F32) * 0.5).astype(BF16)
     heads = h_ref[...].astype(F32)
     gap = jnp.zeros((SLOT - classes, model), F32)
     hc = jnp.concatenate([heads[:, 0], gap, heads[:, 1], gap], axis=0)
@@ -83,13 +85,13 @@
 
     def project(i, c):
         if i < nblk:
-            p_s[block(i), chunk(c)] = jnp.dot(x_s[block(i), :], w1_ref[:, chunk(c)], preferred_element_type=F32)
+            p_s[block(i), chunk(c)] = jnp.dot(x_s[block(i), :], w1h_s[:, chunk(c)], preferred_element_type=F32)
 
     def activate(i, c):
         if i < nblk:
             p = p_s[block(i), chunk(c)]
-            t = jnp.tanh(p * (C0 + (C0 * C1) * (p * p)))
-            a_s[block(i), chunk(c)] = (p * (0.5 + 0.5 * t)).astype(BF16)
+            t = jnp.tanh(p * (2 * C0 + (8 * C0 * C1) * (p * p)))
+            a_s[block(i), chunk(c)] = (p * (1.0 + t)).astype(BF16)
 
     def residual(i):
         if 0 <= i < nblk:
@@ -117,6 +119,14 @@
             tok = block(i)
             dzt_s[:, tok] = jnp.dot(hbt_s[...], e_s[:, tok], preferred_element_type=F32).astype(BF16)
 
+    def back(i):
+        if 0 <= i < nblk:
+            tok = block(i)
+            for t in range(2):
+                row = slice(t * SLOT, (t + 1) * SLOT)
+                dz_s[t, tok, :] = lax.dot_general(
+                    e_s[row, tok], hc_s[row, :], TN, preferred_element_type=F32).astype(BF16)
+
     enter(0)
     for c in range(nchunk):
         project(0, c)
@@ -129,65 +139,82 @@
             project(i + 1, c)
         errors(i - 1)
         back_t(i - 2)
-        if i == nblk // 2 + 1:
+        back(i - 2)
+        if i == min(3, nblk):
             pl.semaphore_wait(barrier, n - 1)
             for c in cnt_copies:
                 c.start()
 
-    def w2_part(c, carry):
-        acc_s[:, chunk(c)] = jnp.dot(dzt_s[...], a_s[:, chunk(c)], preferred_element_type=F32)
-        return carry
-
-    lax.fori_loop(0, nchunk, w2_part, 0)
-
-    for c in cnt_copies:
-        c.wait()
-    cnt_recv[me] = cnt_send[...]
-    tot = cnt_recv[0]
-    for j in range(1, n):
-        tot += cnt_recv[j]
-    inv = 1.0 / jnp.maximum(tot.sum(axis=1, keepdims=True), 1.0)
-    inv0, inv1 = inv[0:1], inv[1:2]
-
-    for c in range(nchunk):
-        f = slice(c * fc, (c + 1) * fc)
-        d = acc_s[:, f]
+    @pl.when(me != n)
+    def _():
+        for c in cnt_copies:
+            c.wait()
+        cnt_recv[me] = cnt_send[...]
+        tot = cnt_recv[0]
+        for j in range(1, n):
+            tot += cnt_recv[j]
+        inv = 1.0 / jnp.maximum(tot.sum(axis=1, keepdims=True), 1.0)
+        inv_s[...] = jnp.broadcast_to(inv, (8, LANES))
+
+    my_y, my_x, my_c = me // 4, (me // 2) % 2, me % 2
+
+    def order(s):
+        return my_y * s + (1 - my_y) * (nchunk - 1 - s)
+
+    def w2_products(s):
+        acc_s[s % 2] = jnp.dot(dzt_s[...], a_s[:, chunk(order(s))], preferred_element_type=F32)
+
+    def w2_scale(s):
+        inv0, inv1 = inv_s[0:1, 0:1], inv_s[1:2, 0:1]
+        d = acc_s[s % 2]
         tail = 2 * LANES + (model - LANES)
         d = jnp.concatenate([d[:LANES] * inv0, d[LANES:2 * LANES] * inv1,
                              d[2 * LANES:tail] * inv0, d[tail:] * inv1], axis=0)
-        send2[f, :] = d.T.astype(BF16)
+        send2[chunk(order(s)), :] = d.T.astype(BF16)
 
     def rows_of(peer):
         return send2.at[pl.ds(pl.multiple_of(peer * rows_out, rows_out), rows_out)]
 
     out_copies = copies(1, rows_of, recv2.at[me])
-    for c in out_copies:
-        c.start()
+
+    def w2_send(s):
+        if s == nchunk - 1:
+            for k in (2, 3, 1):
+                out_copies[k - 1].start()
+            return
+        to_x = (1 - my_y) * (1 - s) + my_y * s
+        for to_c in range(2):
+            peer = (1 - my_y) * 4 + to_x * 2 + to_c
+            k = 4 + 2 * ((my_x + to_x) % 2) + (my_c + to_c) % 2
+            pltpu.make_async_remote_copy(
+                src_ref=rows_of(peer), dst_ref=recv2.at[me], send_sem=send_sem.at[1, k],
+                recv_sem=recv_sem.at[1, k], device_id=(peer,), device_id_type=MESH).start()
+
+    for s in range(nchunk + 1):
+        @pl.when(me != n + 1 + s)
+        def _():
+            if s > 0:
+                w2_scale(s - 1)
+                w2_send(s - 1)
+            if s < nchunk:
+                w2_products(s)
+
+    inv0, inv1 = inv_s[0:1, 0:1], inv_s[1:2, 0:1]
 
     def copies_in(c):
         return copies(2 + c, lambda peer: send1.at[c, peer], recv1.at[c, me])
-
-    def back(i, carry):
-        tok = pl.ds(pl.multiple_of(i * 2 * tb, 2 * tb), 2 * tb)
-        for t in range(2):
-            row = slice(t * SLOT, (t + 1) * SLOT)
-            dz_s[t, tok, :] = lax.dot_general(
-                e_s[row, tok], hc_s[row, :], TN, preferred_element_type=F32).astype(BF16)
-        return carry
-
-    lax.fori_loop(0, nblk // 2, back, 0)
 
     def w1_part(c, carry):
         for i in range(nblk):
             for t in range(2):
-                da = jnp.dot(dz_s[t, block(i), :], w2t_ref[:, chunk(c)], preferred_element_type=F32)
+                da = jnp.dot(dz_s[t, block(i), :], w2h_s[:, chunk(c)], preferred_element_type=F32)
                 for r in range(0, tb, rp):
                     rows = slice(i * tb + r, i * tb + r + rp)
                     if t == 0:
                         p = p_s[rows, chunk(c)]
                         p2 = p * p
-                        h = 0.5 + 0.5 * jnp.tanh(p * (C0 + (C0 * C1) * p2))
-                        sl = h + (p * h * (1.0 - h)) * (2 * C0 + (6 * C0 * C1) * p2)
+                        th = jnp.tanh(p * (2 * C0 + (8 * C0 * C1) * p2))
+                        sl = (1.0 + th) * (1.0 + p * ((1.0 - th) * (2 * C0 + (24 * C0 * C1) * p2)))
                         sl_s[r:r + rp, :] = sl
                     else:
                         sl = sl_s[r:r + rp, :]
@@ -197,8 +224,9 @@
         for j in range(n):
             r = slice(j * rows_in, (j + 1) * rows_in)
             send1[c, j] = jnp.concatenate([d0[r], d1[r]], axis=0).astype(BF16)
-        for cp in copies_in(c):
-            cp.start()
+        now = copies_in(c)
+        for k in (6, 7, 4, 5, 2, 3, 1):
+            now[k - 1].start()
         return carry
 
     lax.fori_loop(0, nchunk, w1_part, 0)
@@ -274,14 +302,13 @@
     g00, g01, g11 = gram[0:1], gram[1:2], gram[2:3]
     scale = 1.0 / ((g00 + g11) * 0.5)
     b0, b1 = (g00 - g01) * scale, (g01 - g11) * scale
-    gap = jnp.zeros((1, LANES), F32)
-    a0 = jnp.full((1, LANES), 0.5, F32)
-    a1 = a0
+    shift, turn = 0.25 * (b0 + b1), 0.25 * (b1 - b0)
+    h = jnp.zeros((1, LANES), F32)
     for _ in range(SOLVER_STEPS):
-        gap = gap + (b0 * a0 + b1 * a1)
-        ratio = jnp.exp(gap)
-        a0 = 1.0 / (1.0 + ratio)
-        a1 = ratio * a0
+        h = (h + shift) + turn * jnp.tanh(h)
+    ratio = jnp.exp(h + h)
+    a0 = 1.0 / (1.0 + ratio)
+    a1 = ratio * a0
     alpha_ref[0] = a0[0, 0]
     alpha_ref[1] = a1[0, 0]
     gin_ref[...] = a0 * u0_ref[0] + a1 * u1_ref[0]
@@ -315,7 +342,10 @@
                 pltpu.VMEM((2, tokens, model), BF16),
                 pltpu.VMEM((2 * model, tokens), BF16),
                 pltpu.VMEM((tokens, model), BF16),
-                pltpu.VMEM((2 * model, hidden), F32),
+                pltpu.VMEM((2, 2 * model, fc), F32),
+                pltpu.VMEM((8, LANES), F32),
+                pltpu.VMEM((model, hidden), BF16),
+                pltpu.VMEM((model, hidden), BF16),
                 pltpu.VMEM((2, tokens, fc), BF16),
                 pltpu.VMEM((hidden, model), BF16),
                 pltpu.VMEM((2 * SLOT, model), BF16),

time: 37.5 us -> 36.7 us (0.979)
  Pallas kernels: 36.7 us -> 35.8 us
    pallas_call x1, Pallas kernels: 34.6 us -> 33.8 us  [local_step(): pl.pallas_call(functools.partial(kernel, n, tb, rp, fc), out_shape=(jax.S...]
where the time goes in v4:
time: 36.7 us; the launch traced here: 36.6 us
  Pallas kernels  35.8 us (98%)
  between operations  0.8 us (2%)
    pallas_call x1, Pallas kernels, local_step(): pl.pallas_call(functools.partial(kernel, n, tb, rp, fc), out_shape=(jax.S...  33.8 us
    pallas_call x1, Pallas kernels, local_step(): pl.pallas_call(finish, out_shape=(jax.ShapeDtypeStruct((2,), F32), jax.Sh...  1.96 us

profile of v4, /device:TPU:0, one launch (start us, length us, event | category | flops | bytes accessed | tf_op | source)
XLA Modules:
  0.0 36.6 jit_solution(5303290975774955452)
XLA Ops:
  0.6 33.8 %shard_map.85 = (f32[2,144,128]{2,1,0:T(8,128)}, f32[2,144,128]{2,1,0:T(8,128)}, f32[8,128]{1,0:T(8,128)}) custom-call(bf16[192,4096]{1,0:T(8,128)(2,1)} %bitcast.5, bf16[192,768]{1,0:T(8,128)(2,1)} %w1_ref.1, bf16[192,768]{1,0:T(8,128)(2,1)} %bitcast.6, bf16[10,2,192]{2,1,0:T(2,128)(2,1)} %bitcast.7, s32[2,4096]{1,0:T(2,128)} %lab_ref.1, s32[2,4096]{1,0:T(2,128)} %mask_ref.1), custom_call_target="tpu_custom_call" | custom-call | tf_op jit(solution)/shard_map/pallas_call | solution.py:329
  34.4 2.0 %shard_map.86 = (f32[2]{0:T(128)}, f32[144,128]{1,0:T(8,128)}, f32[144,128]{1,0:T(8,128)}) custom-call(f32[2,144,128]{2,1,0:T(8,128)} %get-tuple-element.9.u0_ref, f32[2,144,128]{2,1,0:T(8,128)} %get-tuple-element.10.u1_ref, f32[8,128]{1,0:T(8,128)} %get-tuple-element.11.gram_ref), custom_call_target="tpu_custom_call" | custom-call | tf_op jit(solution)/shard_map/pallas_call | solution.py:369
